TPU v7x, 32 devices: a 4x4x1 block of a 4x4x8 slice. The times are simulated.
32 devices in a mesh: dp: 1 (over z), col: 4 (over y), row: 8 (over x, core).
Axes of the slice: x: 4, y: 4, z: 1, core: 2. Of those that a mesh axis runs over, the one named last changes fastest.
The devices are a block of a 4x4x8 slice.
Arguments:
- pair_rep: bfloat16 [1536, 1536, 64], P(('dp', 'row'), 'col')
- pair_mask: int32 [1536, 1536], P(('dp', 'row'), 'col')
- norm_in: bfloat16 [64], replicated
- proj_left: bfloat16 [64, 64], replicated
- gate_left: bfloat16 [64, 64], replicated
- proj_right: bfloat16 [64, 64], replicated
- gate_right: bfloat16 [64, 64], replicated
- proj_gate: bfloat16 [64, 64], replicated
- norm_out: bfloat16 [64], replicated
- proj_out: bfloat16 [64, 64], replicated
Outputs:
- output: bfloat16 [1536, 1536, 64], P(('dp', 'row'), 'col')
All inputs are finite; a program needn't handle non-finite values.
Results may differ from a plain program's by a relative error of at most 0.00624021.
Values are sent between devices in bfloat16 or wider.
A program may use at most 768 MiB of HBM per device.

v0:
```python
import jax
import jax.numpy as jnp
from jax import lax
from jax.sharding import PartitionSpec as P

LN_EPS = 1e-5


def layer_norm(values, gain_vec, red_axis):
    centre = values - jnp.mean(values, axis=red_axis, keepdims=True)
    spread = jnp.mean(centre * centre, axis=red_axis, keepdims=True)
    return centre * lax.rsqrt(spread + LN_EPS) * gain_vec


def tile_front(pair_tile, mask_tile, norm_in, w_concat, proj_gate):
    hidden = w_concat.shape[1] // 4
    pair_f = pair_tile.astype(jnp.float32)
    normed = layer_norm(pair_f, norm_in.astype(jnp.float32), -1).astype(jnp.bfloat16)
    projected = jnp.einsum('ijd,de->eij', normed, w_concat, preferred_element_type=jnp.float32)
    keep_f = mask_tile.astype(jnp.float32)
    left_op = (keep_f * jax.nn.sigmoid(projected[hidden:2 * hidden]) * projected[:hidden]).astype(jnp.bfloat16)
    right_op = (keep_f * jax.nn.sigmoid(projected[3 * hidden:]) * projected[2 * hidden:3 * hidden]).astype(jnp.bfloat16)
    out_gate = jax.nn.sigmoid(jnp.dot(normed, proj_gate, preferred_element_type=jnp.float32))
    return left_op, right_op, out_gate, pair_f


def tile_back(contracted, pair_f, out_gate, norm_out, proj_out):
    normed_o = layer_norm(contracted, norm_out.astype(jnp.float32)[:, None, None], 0).astype(jnp.bfloat16)
    update = jnp.einsum('cij,cd->ijd', normed_o, proj_out, preferred_element_type=jnp.float32)
    return (pair_f + out_gate * update).astype(jnp.bfloat16)


def solution(mesh):
    grid_rows = mesh.shape['row']
    grid_cols = mesh.shape['col']
    row_ratio = grid_rows // grid_cols
    swap_pairs = [
        (src_col * grid_rows + src_row,
         (src_row // row_ratio) * grid_rows + (src_row % row_ratio) * grid_cols + src_col)
        for src_row in range(grid_rows) for src_col in range(grid_cols)
    ]
    tile_spec = P(('dp', 'row'), 'col', None)
    mask_spec = P(('dp', 'row'), 'col')

    def tile_program(pair_tile, mask_tile, norm_in, proj_left, gate_left, proj_right, gate_right, proj_gate, norm_out, proj_out):
        w_concat = jnp.concatenate([proj_left, gate_left, proj_right, gate_right], axis=1)
        left_op, right_op, out_gate, pair_f = tile_front(pair_tile, mask_tile, norm_in, w_concat, proj_gate)
        hidden, tile_rows, tile_cols = left_op.shape
        left_full = lax.all_gather(left_op, 'col', axis=2, tiled=True)
        right_moved = lax.ppermute(right_op, ('col', 'row'), swap_pairs)
        right_full = lax.all_gather(right_moved, 'row', axis=2, tiled=True)
        seq_len = left_full.shape[2]
        right_full = right_full.reshape(hidden, tile_rows, row_ratio, seq_len)
        contracted = jnp.einsum('cin,crpn->cipr', left_full, right_full, preferred_element_type=jnp.float32)
        contracted = contracted.reshape(hidden, tile_rows, tile_cols)
        return tile_back(contracted, pair_f, out_gate, norm_out, proj_out)

    return jax.shard_map(tile_program, mesh=mesh, in_specs=(tile_spec, mask_spec) + (P(),) * 8, out_specs=tile_spec, check_vma=False)
```

profile of v0, /device:TPU:97, one launch (start us, length us, event | category | flops | bytes accessed | tf_op | source)
XLA Modules:
  0.0 1169.0 jit_solution(15054950560945783438)
XLA Ops:
  6.5 0.0 copy-start
  6.6 0.0 copy-start.13
  6.6 0.0 copy-start.5
  6.6 0.0 copy-start.9
  6.6 0.0 copy-start.8
  6.6 0.0 copy-start.7
  6.6 0.0 copy-start.6
  6.6 0.1 all-gather.3.cloned.1.call-start
  6.7 7.3 convert_reduce_fusion
  13.9 0.0 copy-start.1
  14.0 8.1 fusion.7
  22.1 0.0 copy-done.13
  22.1 0.0 copy-start.3
  22.2 0.0 copy-done.5
  22.2 0.0 copy-start.10
  22.2 0.0 copy-done.9
  22.2 0.0 copy-done.8
  22.2 0.0 copy-done.7
  22.2 0.0 copy-done.6
  22.2 30.3 %fusion.25 = f32[256,192,384]{2,0,1:T(8,128)} fusion(bf16[192,384,64]{1,2,0:T(8,128)(2,1)} %param.10, f32[64]{0:T(128)S(1)} %convert_element_type.28, f32[192,384]{1,0:T(8,128)S(1)} %add_rsqrt_fusion.1, f32[192,384]{1,0:T(8,128)S(1)} %broadcast_multiply_fusion.1, bf16[64,64]{1,0:T(8,128)(2,1)S(1)} %copy-done.6, bf16[64,64]{1,0:T(8,128)(2,1)S(1)} %copy-done.7, ...), kind=kOutput, calls=%fused_computation.35 | convolution fusion | flops 2439643136 | bytes 85557504 | tf_op jit(solution)/shard_map/ijd,de->eij/dot_general | solution.py:19
  52.5 0.0 copy-done.1
  52.5 0.0 copy-done.3
  52.5 0.0 copy-done.10
  52.5 29.2 %fusion.11 = (bf16[64,192,384]{2,0,1:T(8,128)(2,1)}, bf16[64,192,384]{2,0,1:T(8,128)(2,1)S(1)}) fusion(f32[256,192,384]{2,0,1:T(8,128)} %fusion.25, f32[192,384]{1,0:T(8,128)S(1)} %convert_element_type.30), kind=kLoop, calls=%fused_computation.17 | loop fusion | flops 56623104 | bytes 94666752 | tf_op jit(solution)/shard_map/convert_element_type | solution.py:21
  81.8 0.0 copy-start.14
  81.8 6.4 collective-permute-start
  88.2 196.9 %collective-permute-done = bf16[64,192,384]{2,0,1:T(8,128)(2,1)} collective-permute-done((bf16[64,192,384]{2,0,1:T(8,128)(2,1)S(1)}, bf16[64,192,384]{2,0,1:T(8,128)(2,1)}, u32[]{:S(2)}, u32[]{:S(2)}) %collective-permute-start) | collective-permute-done | bytes 9437216 | tf_op jit(solution)/shard_map/ppermute | solution.py:50
  285.0 0.1 all-gather.3.cloned.1.call-update
  285.1 0.1 all-gather.5.cloned.1.call-start
  285.2 0.7 all-gather.5.cloned.1.call-update
  285.9 0.0 copy-done.14
  285.9 340.4 %all-gather.3.cloned.1.call-done = bf16[64,192,3072]{2,0,1:T(8,128)(2,1)} async-done(((bf16[64,192,384]{2,0,1:T(8,128)(2,1)}), bf16[64,192,3072]{2,0,1:T(8,128)(2,1)}) %all-gather.3.cloned.1.call-update) | async-done | bytes 75497488 | tf_op jit(solution)/shard_map/all_gather | solution.py:51
  626.3 162.1 %reshape.50 = bf16[64,192,2,1536]{3,2,0,1:T(2,128)(2,1)} reshape(bf16[64,192,3072]{2,0,1:T(8,128)(2,1)} %all-gather.3.cloned.1.call-done) | data formatting | bytes 150994944 | tf_op jit(solution)/shard_map/reshape | solution.py:53
  788.4 165.2 %all-gather.5.cloned.1.call-done = bf16[64,192,1536]{2,0,1:T(8,128)(2,1)} async-done(((bf16[64,192,384]{2,0,1:T(8,128)(2,1)}), bf16[64,192,1536]{2,0,1:T(8,128)(2,1)}) %all-gather.5.cloned.1.call-update) | async-done | bytes 37748752 | tf_op jit(solution)/shard_map/all_gather | solution.py:49
  953.7 138.8 %bitcast_reduce_fusion = (f32[192,2,192]{0,2,1:T(8,128)S(1)}, f32[64,192,2,192]{3,1,2,0:T(8,128)}) fusion(bf16[64,192,1536,1]{2,0,1,3:T(8,128)(2,1)} %bitcast.26, bf16[64,192,2,1536]{3,2,0,1:T(2,128)(2,1)} %reshape.50), kind=kOutput, calls=%fused_computation.6 | convolution fusion | flops 14500159488 | bytes 132415488 | tf_op jit(solution)/shard_map/cin,crpn->cipr/dot_general | solution.py:54
  1092.5 9.9 fusion.4
  1102.4 0.1 add_rsqrt_fusion
  1102.5 0.1 copy.16
  1102.6 23.1 %copy.15 = f32[64,192,384]{2,0,1:T(8,128)} copy(f32[64,192,384]{1,2,0:T(8,128)} %bitcast.23) | data formatting | bytes 37748736 | tf_op jit(solution)/shard_map/reshape | solution.py:55
  1125.8 0.1 copy.14
  1125.9 0.0 copy-done
  1125.9 0.0 copy-start.2
  1125.9 0.0 copy-start.4
  1125.9 0.0 copy-start.11
  1125.9 0.0 copy-start.12
  1126.0 15.9 %fusion.21 = f32[192,384,64]{1,2,0:T(8,128)} fusion(f32[64,192,384]{2,0,1:T(8,128)} %copy.15, f32[64]{0:T(128)S(1)} %convert_element_type.33, f32[192,384]{1,0:T(8,128)S(1)} %copy.16, f32[192,384]{1,0:T(8,128)S(1)} %copy.14, bf16[64,64]{1,0:T(8,128)(2,1)S(1)} %copy-done), kind=kOutput, calls=%fused_computation.31 | convolution fusion | flops 622854144 | bytes 38347008 | tf_op jit(solution)/shard_map/cij,cd->ijd/dot_general | solution.py:29
  1141.8 0.0 copy-done.2
  1141.8 0.0 copy-done.4
  1141.8 0.0 copy-done.11
  1141.8 0.0 copy-done.12
  1141.8 19.9 %fusion.10 = bf16[192,384,64]{1,2,0:T(8,128)(2,1)} fusion(bf16[192,384,64]{1,2,0:T(8,128)(2,1)} %param.10, f32[192,384,64]{1,2,0:T(8,128)} %fusion.21, f32[64]{0:T(128)S(1)} %copy-done.11, f32[192,384]{1,0:T(8,128)S(1)} %copy-done.4, f32[192,384]{1,0:T(8,128)S(1)} %copy-done.2, bf16[64,64]{1,0:T(8,128)(2,1)S(1)} %copy-done.12), kind=kOutput, calls=%fused_computation.15 | convolution fusion | flops 660602880 | bytes 38347008 | tf_op jit(solution)/shard_map/dot_general | solution.py:23
  (6 shorter events, 0.1 us)
Async XLA Ops:
  6.5 1119.4 %copy-start = (bf16[64,64]{1,0:T(8,128)(2,1)S(1)}, bf16[64,64]{1,0:T(8,128)(2,1)}, u32[]{:S(2)}) copy-start(bf16[64,64]{1,0:T(8,128)(2,1)} %param.19) | copy-start | bytes 24580
  6.6 15.6 %copy-start.13 = (bf16[64]{0:T(256)(128)(2,1)S(1)}, bf16[64]{0:T(256)(128)(2,1)}, u32[]{:S(2)}) copy-start(bf16[64]{0:T(256)(128)(2,1)} %param.12) | copy-start | bytes 388
  6.6 15.6 %copy-start.5 = (s32[192,384]{1,0:T(8,128)S(1)}, s32[192,384]{1,0:T(8,128)}, u32[]{:S(2)}) copy-start(s32[192,384]{1,0:T(8,128)} %param.11) | copy-start | bytes 884740
  6.6 15.7 %copy-start.9 = (bf16[64,64]{1,0:T(8,128)(2,1)S(1)}, bf16[64,64]{1,0:T(8,128)(2,1)}, u32[]{:S(2)}) copy-start(bf16[64,64]{1,0:T(8,128)(2,1)} %param.13) | copy-start | bytes 24580
  6.6 15.7 %copy-start.8 = (bf16[64,64]{1,0:T(8,128)(2,1)S(1)}, bf16[64,64]{1,0:T(8,128)(2,1)}, u32[]{:S(2)}) copy-start(bf16[64,64]{1,0:T(8,128)(2,1)} %param.14) | copy-start | bytes 24580
  6.6 15.7 %copy-start.7 = (bf16[64,64]{1,0:T(8,128)(2,1)S(1)}, bf16[64,64]{1,0:T(8,128)(2,1)}, u32[]{:S(2)}) copy-start(bf16[64,64]{1,0:T(8,128)(2,1)} %param.15) | copy-start | bytes 24580
  6.6 15.7 %copy-start.6 = (bf16[64,64]{1,0:T(8,128)(2,1)S(1)}, bf16[64,64]{1,0:T(8,128)(2,1)}, u32[]{:S(2)}) copy-start(bf16[64,64]{1,0:T(8,128)(2,1)} %param.16) | copy-start | bytes 24580
  6.6 619.7 %all-gather.3.cloned.1.call-start = ((), (), s32[]{:S(2)}) async-start(), calls=%async_computation | async-start | bytes 84934656 | tf_op jit(solution)/shard_map/all_gather | solution.py:51
  13.9 38.6 %copy-start.1 = (f32[192,384]{1,0:T(8,128)}, f32[192,384]{1,0:T(8,128)S(1)}, u32[]{:S(2)}) copy-start(f32[192,384]{1,0:T(8,128)S(1)} %broadcast_multiply_fusion.1) | copy-start | bytes 884740
  22.1 30.4 %copy-start.3 = (f32[192,384]{1,0:T(8,128)}, f32[192,384]{1,0:T(8,128)S(1)}, u32[]{:S(2)}) copy-start(f32[192,384]{1,0:T(8,128)S(1)} %add_rsqrt_fusion.1) | copy-start | bytes 884740
  22.2 30.3 %copy-start.10 = (f32[64]{0:T(128)}, f32[64]{0:T(128)S(1)}, u32[]{:S(2)}) copy-start(f32[64]{0:T(128)S(1)} %convert_element_type.28) | copy-start | bytes 772
  81.8 204.2 %copy-start.14 = (bf16[64]{0:T(256)(128)(2,1)S(1)}, bf16[64]{0:T(256)(128)(2,1)}, u32[]{:S(2)}) copy-start(bf16[64]{0:T(256)(128)(2,1)} %param.18) | copy-start | bytes 388
  81.8 203.3 %collective-permute-start = (bf16[64,192,384]{2,0,1:T(8,128)(2,1)S(1)}, bf16[64,192,384]{2,0,1:T(8,128)(2,1)}, u32[]{:S(2)}, u32[]{:S(2)}) collective-permute-start(bf16[64,192,384]{2,0,1:T(8,128)(2,1)S(1)} %get-tuple-element.6), channel_id=1, source_target_pairs={{0,0},{8,1},{16,2},{24,3},{1,4},{9,5},{17,6},{25,7},{2,8},{10,9},{... | collective-permute-start | bytes 28311560 | tf_op jit(solution)/shard_map/ppermute | solution.py:50
  285.1 668.6 %all-gather.5.cloned.1.call-start = ((), (), s32[]{:S(2)}) async-start(), calls=%async_computation.1 | async-start | bytes 47185920 | tf_op jit(solution)/shard_map/all_gather | solution.py:49
  1125.9 15.9 %copy-start.2 = (f32[192,384]{1,0:T(8,128)S(1)}, f32[192,384]{1,0:T(8,128)}, u32[]{:S(2)}) copy-start(f32[192,384]{1,0:T(8,128)} %copy-done.1) | copy-start | bytes 884740
  1125.9 15.9 %copy-start.4 = (f32[192,384]{1,0:T(8,128)S(1)}, f32[192,384]{1,0:T(8,128)}, u32[]{:S(2)}) copy-start(f32[192,384]{1,0:T(8,128)} %copy-done.3) | copy-start | bytes 884740
  1125.9 15.9 %copy-start.11 = (f32[64]{0:T(128)S(1)}, f32[64]{0:T(128)}, u32[]{:S(2)}) copy-start(f32[64]{0:T(128)} %copy-done.10) | copy-start | bytes 772
  1125.9 15.9 %copy-start.12 = (bf16[64,64]{1,0:T(8,128)(2,1)S(1)}, bf16[64,64]{1,0:T(8,128)(2,1)}, u32[]{:S(2)}) copy-start(bf16[64,64]{1,0:T(8,128)(2,1)} %param.17) | copy-start | bytes 24580
Sparse Core Ops, SparseCore 0:
  285.2 341.0 all-gather.2
  627.9 325.7 all-gather.4
where the time goes:
time: 1180 us; the launch traced here: 1170 us
  waiting for transfers between devices  703 us (60%)
  matrix products  205 us (17%)
  local copies, waits for them, and re-layouts  186 us (16%)
  other arithmetic  54.7 us (5%)
  between operations  14.1 us (1%)
    all_gather x1, waiting for transfers between devices, tile_program(): right_full = lax.all_gather(right_moved, 'row', axis=2, tiled=True)  340 us
    ppermute x1, waiting for transfers between devices, tile_program(): right_moved = lax.ppermute(right_op, ('col', 'row'), swap_pairs)  197 us
    all_gather x1, waiting for transfers between devices, tile_program(): left_full = lax.all_gather(left_op, 'col', axis=2, tiled=True)  165 us
    reshape x1, local copies, waits for them, and re-layouts, tile_program(): right_full = right_full.reshape(hidden, tile_rows, row_ratio, seq_len)  162 us
    dot_general x1, matrix products, tile_program(): jnp.einsum('cin,crpn->cipr', left_full, right_full, preferred_element_typ...  139 us
    dot_general x1, matrix products, tile_front(): jnp.einsum('ijd,de->eij', normed, w_concat, preferred_element_type=jnp.fl...  30.3 us
    convert_element_type x1, other arithmetic, tile_front(): (keep_f * jax.nn.sigmoid(projected[hidden:2 * hidden]) * projected[:hidde...  29.2 us
  transfers between devices with their start and end apart: 3, of which 3 were waited for; matrix products, arithmetic and copies ran while one was open for 14% of the time, Pallas kernels for 0%

commit v1 on v0

v1 whole, which is shorter than its diff:
```python
import functools

import jax
import jax.numpy as jnp
from jax import lax
from jax.experimental import pallas as pl
from jax.experimental.pallas import tpu as pltpu
from jax.sharding import PartitionSpec as P

LN_EPS = 1e-5
F32 = jnp.float32
BF16 = jnp.bfloat16
MESH = pl.DeviceIdType.MESH
VMEM_LIMIT = 60 * 1024 * 1024
PER_HALF = 1
FRONT_ROWS = 16


def normalize(values, gain):
    centre = values - jnp.mean(values, axis=0, keepdims=True)
    spread = jnp.mean(centre * centre, axis=0, keepdims=True)
    return (centre * lax.rsqrt(spread + LN_EPS) * gain).astype(BF16)


def front_kernel(z_ref, m_ref, g_ref, w_ref, a_ref, b_ref, sa, sb):
    rows, chan, cols = z_ref.shape
    tiles = sa.shape[0]
    pitch = sa.shape[1] // rows
    hid = w_ref.shape[0] // 4

    def one_row(i, _):
        xn = normalize(z_ref[i].astype(F32), g_ref[...])
        p = jnp.dot(w_ref[...], xn, preferred_element_type=F32)
        keep = m_ref[pl.ds(i, 1), :].astype(F32)
        left = keep * jax.nn.sigmoid(p[hid:2 * hid]) * p[:hid]
        right = keep * jax.nn.sigmoid(p[3 * hid:]) * p[2 * hid:3 * hid]
        at = pl.ds(pl.multiple_of(i * pitch, 8), hid)
        for t in range(tiles):
            sa[t, at, :] = left[:, t * 128:(t + 1) * 128]
            sb[t, at, :] = right[:, t * 128:(t + 1) * 128]
        return 0

    lax.fori_loop(0, rows, one_row, 0, unroll=2)

    def one_channel(c, _):
        for t in range(tiles):
            at = slice(t * 128, (t + 1) * 128)
            a_ref[c, :, at] = sa[t, pl.ds(c, rows, stride=pitch), :].astype(BF16)
            b_ref[c, :, at] = sb[t, pl.ds(c, rows, stride=pitch), :].astype(BF16)
        return 0

    lax.fori_loop(0, hid, one_channel, 0, unroll=4)


def front(z_t, mask, g_in, w_cat):
    rows, chan, cols = z_t.shape
    hid = w_cat.shape[0] // 4
    fr = FRONT_ROWS
    scratch = pltpu.VMEM((cols // 128, fr * (hid + 8), 128), F32)
    out = jax.ShapeDtypeStruct((hid, rows, cols), BF16)
    out_spec = pl.BlockSpec((hid, fr, cols), lambda i: (0, i, 0))
    return pl.pallas_call(
        front_kernel,
        grid=(rows // fr,),
        in_specs=[
            pl.BlockSpec((fr, chan, cols), lambda i: (i, 0, 0)),
            pl.BlockSpec((fr, cols), lambda i: (i, 0)),
            pl.BlockSpec((chan, 1), lambda i: (0, 0)),
            pl.BlockSpec(w_cat.shape, lambda i: (0, 0)),
        ],
        out_specs=[out_spec, out_spec],
        out_shape=[out, out],
        scratch_shapes=[scratch, scratch],
        compiler_params=pltpu.CompilerParams(vmem_limit_bytes=VMEM_LIMIT),
        name="front",
    )(z_t, mask, g_in, w_cat)


def main_kernel(nc, a_own, b_own, z_hbm, g_in, w_gate, g_out, w_out, out_hbm, a_land, b_land,
                a_buf, b_buf, o_buf, z_buf, sem_sp, sem_rp, sem_sa, sem_ra, sem_se, sem_re,
                sem_sd, sem_rd, sem_l, sem_z):
    hid, rows, cols = a_own.shape
    h = PER_HALF
    ch = 2 * h
    n = hid // ch
    half = hid // 2
    relay0 = 8 * hid
    dp, y, r = lax.axis_index("dp"), lax.axis_index("col"), lax.axis_index("row")
    cores = 2
    x, core = r // cores, r % cores
    up = lambda v: (v + 1) % nc
    dn = lambda v: (v + nc - 1) % nc
    xp, xm = (dp, y, up(x) * cores + core), (dp, y, dn(x) * cores + core)
    yp, ym = (dp, up(y), r), (dp, dn(y), r)
    mate = (dp, y, x * cores + 1 - core)
    cls = (y + nc - x) % nc
    is0 = cls == 0
    eq = [(cls == k).astype(jnp.int32) for k in range(4)]
    pick = lambda c0, c1, c2, c3: eq[0] * c0 + eq[1] * c1 + eq[2] * c2 + eq[3] * c3

    barrier = pltpu.get_barrier_semaphore()
    for dev in (xp, xm, yp, ym, mate):
        pl.semaphore_signal(barrier, inc=1, device_id=dev, device_id_type=MESH)
    pl.semaphore_wait(barrier, 5)

    load_z = pltpu.make_async_copy(z_hbm, z_buf, sem_z.at[0])
    load_z.start()

    dirs = [pick(1, 3, 0, 2), pick(0, 1, 1, 0), pick(2, 0, 3, 1), pick(3, 2, 2, 3)]
    hops = [pick(2, 1, 1, 1), pick(2, 1, 1, 1), pick(3, 2, 2, 2), pick(3, 4, 2, 4)]
    src_relay = [3, 2, pick(0, 0, 1, 1), pick(1, 2, 0, 3)]
    tgt = [pick(4, 3, 0, 2), pick(4, 1, 1, 0), pick(2, 0, 5, 1), pick(3, 4, 5, 5)]

    def dev_of(d):
        dx = (d == 0).astype(jnp.int32) + 3 * (d == 1).astype(jnp.int32)
        dy = (d == 2).astype(jnp.int32) + 3 * (d == 3).astype(jnp.int32)
        return (dp, (y + dy) % nc, ((x + dx) % nc) * cores + core)

    perm_devs = [dev_of(d) for d in dirs]

    def tgt_at(k, t):
        to_e = tgt[k] // 4
        return (1 - to_e) * (relay0 + tgt[k] * half + t * h) + to_e * ((2 * t + tgt[k] - 4) * h)

    def remote(src, dst, send, recv, dev):
        return pltpu.make_async_remote_copy(src_ref=src, dst_ref=dst, send_sem=send, recv_sem=recv,
                                            device_id=dev, device_id_type=MESH)

    def perm_copy(k, t, src):
        return remote(src, b_land.at[pl.ds(tgt_at(k, t), h)], sem_sp.at[k, t], sem_rp.at[tgt[k], t], perm_devs[k])

    def got_perm(which, t):
        pltpu.make_async_copy(b_land.at[pl.ds(0, h)], b_land.at[pl.ds(0, h)], sem_rp.at[which, t]).wait()

    def land(buf, slot, t, f=0, count=ch):
        return buf.at[pl.ds(slot * hid + t * ch + f * h, count)]

    def got(buf, sem, count):
        pltpu.make_async_copy(buf.at[pl.ds(0, count)], buf.at[pl.ds(0, count)], sem).wait()

    def own(buf, t, count=ch, f=0):
        return buf.at[pl.ds(t * ch + f * h, count)]

    def a_own_sends(t):
        return [
            remote(own(a_own, t), land(a_land, 0, t), sem_sa.at[0, t], sem_ra.at[0, t], yp),
            remote(own(a_own, t), land(a_land, 1, t), sem_sa.at[1, t], sem_ra.at[1, t], ym),
        ]

    def e_own_sends(t, src):
        return [
            remote(src, land(b_land, 1, t), sem_se.at[0, t], sem_re.at[0, t], xp),
            remote(src, land(b_land, 2, t), sem_se.at[1, t], sem_re.at[1, t], xm),
            remote(src, land(b_land, 4, t), sem_sd.at[0, t], sem_rd.at[0, t], mate),
        ]

    def local_loads(t, slot):
        put_a = lambda rel: a_buf.at[slot, :, :, pl.ds(rel * cols, cols)]
        out = [
            (own(a_own, t), put_a(0)),
            (land(a_land, 0, t), put_a(3)),
            (land(a_land, 1, t), put_a(1)),
            (land(a_land, 2, t), put_a(2)),
        ]
        for k, delta in enumerate((0, 3, 1, 2)):
            rel = (cls + nc - delta) % nc
            where = pl.ds(pl.multiple_of(rel * cols, 128), cols)
            if k > 0:
                out.append((land(b_land, k, t), b_buf.at[slot, :, core, :, where]))
            out.append((land(b_land, 4 + k, t), b_buf.at[slot, :, 1 - core, :, where]))
        return [pltpu.make_async_copy(s, d, sem_l.at[slot, j]) for j, (s, d) in enumerate(out)]

    def own_e_load(t, slot, src):
        where = pl.ds(pl.multiple_of(cls * cols, 128), cols)
        return pltpu.make_async_copy(src, b_buf.at[slot, :, core, :, where], sem_l.at[slot, 11])

    def at_lag(q, lag, fn):
        t = q - lag

        @pl.when(jnp.logical_and(t >= 0, t < n))
        def _():
            fn(t)

    def step(q, _):
        for k in range(4):
            def send(t, k=k):
                if k < 2:
                    @pl.when(is0)
                    def _():
                        got_perm(src_relay[k], t)
                        perm_copy(k, t, b_land.at[pl.ds(relay0 + src_relay[k] * half + t * h, h)]).start()

                    @pl.when(jnp.logical_not(is0))
                    def _():
                        perm_copy(k, t, own(b_own, t, h, k)).start()
                else:
                    got_perm(src_relay[k], t)
                    perm_copy(k, t, b_land.at[pl.ds(relay0 + src_relay[k] * half + t * h, h)]).start()

            at_lag(q, hops[k] - 1, send)

        def e_own(t):
            @pl.when(is0)
            def _():
                for c in e_own_sends(t, own(b_own, t)):
                    c.start()

            @pl.when(jnp.logical_not(is0))
            def _():
                got_perm(4, t)
                got_perm(5, t)
                for c in e_own_sends(t, land(b_land, 0, t)):
                    c.start()

        at_lag(q, 4, e_own)

        def a_first(t):
            for c in a_own_sends(t):
                c.start()

        at_lag(q, 3, a_first)

        def e_fwd(t):
            got(b_land, sem_re.at[0, t], ch)
            remote(land(b_land, 1, t, 0, h), land(b_land, 3, t, 0, h), sem_se.at[2, t], sem_re.at[2, t], xp).start()
            remote(land(b_land, 1, t), land(b_land, 5, t), sem_sd.at[1, t], sem_rd.at[1, t], mate).start()
            got(b_land, sem_re.at[1, t], ch)
            remote(land(b_land, 2, t, 1, h), land(b_land, 3, t, 1, h), sem_se.at[3, t], sem_re.at[3, t], xm).start()
            remote(land(b_land, 2, t), land(b_land, 6, t), sem_sd.at[2, t], sem_rd.at[2, t], mate).start()

        at_lag(q, 5, e_fwd)

        def a_fwd(t):
            got(a_land, sem_ra.at[0, t], ch)
            remote(land(a_land, 0, t, 0, h), land(a_land, 2, t, 0, h), sem_sa.at[2, t], sem_ra.at[2, t], yp).start()
            got(a_land, sem_ra.at[1, t], ch)
            remote(land(a_land, 1, t, 1, h), land(a_land, 2, t, 1, h), sem_sa.at[3, t], sem_ra.at[3, t], ym).start()

        at_lag(q, 4, a_fwd)

        def last_d2d(t):
            got(b_land, sem_re.at[2, t], h)
            got(b_land, sem_re.at[3, t], h)
            remote(land(b_land, 3, t), land(b_land, 7, t), sem_sd.at[3, t], sem_rd.at[3, t], mate).start()

        at_lag(q, 6, last_d2d)

        def load(t):
            got(a_land, sem_ra.at[2, t], h)
            got(a_land, sem_ra.at[3, t], h)
            for k in range(4):
                got(b_land, sem_rd.at[k, t], ch)
            slot = t % 2
            for c in local_loads(t, slot):
                c.start()

            @pl.when(is0)
            def _():
                own_e_load(t, slot, own(b_own, t)).start()

            @pl.when(jnp.logical_not(is0))
            def _():
                own_e_load(t, slot, land(b_land, 0, t)).start()

        at_lag(q, 7, load)

        def multiply(t):
            slot = t % 2
            for c in local_loads(t, slot):
                c.wait()
            own_e_load(t, slot, land(b_land, 0, t)).wait()
            pitch = o_buf.shape[1] // hid
            for c in range(ch):
                rhs = b_buf[slot, c].reshape(cores * rows, nc * cols)
                prod = lax.dot_general(a_buf[slot, c], rhs, (((1,), (1,)), ((), ())), preferred_element_type=F32)
                at = pl.ds(pl.multiple_of((t * ch + c) * pitch, 8), rows)
                for j in range(o_buf.shape[0]):
                    o_buf[j, at, :] = prod[:, j * 128:(j + 1) * 128]

        at_lag(q, 8, multiply)
        return 0

    lax.fori_loop(0, n + 8, step, 0)

    load_z.wait()
    pitch = o_buf.shape[1] // hid

    def back_row(i, _):
        z = z_buf[i].astype(F32)
        xn = normalize(z, g_in[...])
        gate = jax.nn.sigmoid(jnp.dot(w_gate[...], xn, preferred_element_type=F32))
        o = jnp.concatenate([o_buf[j, pl.ds(i, hid, stride=pitch), :] for j in range(o_buf.shape[0])], axis=1)
        on = normalize(o, g_out[...])
        update = jnp.dot(w_out[...], on, preferred_element_type=F32)
        z_buf[i] = (z + gate * update).astype(BF16)
        return 0

    per = rows // 8
    for blk in range(8):
        lax.fori_loop(blk * per, (blk + 1) * per, back_row, 0, unroll=2)
        pltpu.make_async_copy(z_buf.at[pl.ds(blk * per, per)], out_hbm.at[pl.ds(blk * per, per)], sem_z.at[1 + blk]).start()

    def drain(t, _):
        for k in range(4):
            pltpu.make_async_copy(own(b_own, t, h), own(b_own, t, h), sem_sp.at[k, t]).wait()
            pltpu.make_async_copy(own(b_own, t), own(b_own, t), sem_sd.at[k, t]).wait()
        for k in range(4):
            cnt = ch if k < 2 else h
            pltpu.make_async_copy(own(b_own, t, cnt), own(b_own, t, cnt), sem_sa.at[k, t]).wait()
            pltpu.make_async_copy(own(b_own, t, cnt), own(b_own, t, cnt), sem_se.at[k, t]).wait()
        return 0

    lax.fori_loop(0, n, drain, 0)
    for blk in range(8):
        pltpu.make_async_copy(z_buf.at[pl.ds(blk * per, per)], out_hbm.at[pl.ds(blk * per, per)], sem_z.at[1 + blk]).wait()


def main_call(nc, a_own, b_own, z_t, g_in, w_gate, g_out, w_out):
    hid, rows, cols = a_own.shape
    chan = z_t.shape[1]
    ch = 2 * PER_HALF
    n = hid // ch
    any_spec = pl.BlockSpec(memory_space=pl.ANY)
    vm = pl.BlockSpec(memory_space=pltpu.VMEM)
    dma = lambda *s: pltpu.SemaphoreType.DMA(s)
    return pl.pallas_call(
        functools.partial(main_kernel, nc),
        in_specs=[any_spec] * 3 + [vm] * 4,
        out_specs=[any_spec] * 3,
        out_shape=[
            jax.ShapeDtypeStruct(z_t.shape, BF16),
            jax.ShapeDtypeStruct((3 * hid, rows, cols), BF16),
            jax.ShapeDtypeStruct((10 * hid, rows, cols), BF16),
        ],
        scratch_shapes=[
            pltpu.VMEM((2, ch, rows, nc * cols), BF16),
            pltpu.VMEM((2, ch, 2, rows, nc * cols), BF16),
            pltpu.VMEM((cols // 128, hid * (rows + 8), 128), F32),
            pltpu.VMEM(z_t.shape, BF16),
            dma(4, n), dma(6, n), dma(4, n), dma(4, n), dma(4, n), dma(4, n), dma(4, n), dma(4, n),
            dma(2, 12), dma(9),
        ],
        compiler_params=pltpu.CompilerParams(
            vmem_limit_bytes=VMEM_LIMIT, collective_id=0, has_side_effects=True),
        name="exchange",
    )(a_own, b_own, z_t, g_in, w_gate, g_out, w_out)[0]


def solution(mesh):
    nc = mesh.shape['col']
    tile_spec = P(('dp', 'row'), 'col', None)
    mask_spec = P(('dp', 'row'), 'col')

    def tile_program(pair_tile, mask_tile, norm_in, proj_left, gate_left, proj_right, gate_right, proj_gate, norm_out, proj_out):
        z_t = jnp.transpose(pair_tile, (0, 2, 1))
        w_cat = jnp.concatenate([proj_left, gate_left, proj_right, gate_right], axis=1).T
        g_in = norm_in.astype(F32)[:, None]
        g_out = norm_out.astype(F32)[:, None]
        a_own, b_own = front(z_t, mask_tile, g_in, w_cat)
        out = main_call(nc, a_own, b_own, z_t, g_in, proj_gate.T, g_out, proj_out.T)
        return jnp.transpose(out, (0, 2, 1))

    return jax.shard_map(tile_program, mesh=mesh, in_specs=(tile_spec, mask_spec) + (P(),) * 8, out_specs=tile_spec, check_vma=False)
```

time: 1180 us -> 534 us (0.45)
  waiting for transfers between devices: 703 us -> 0 us
  Pallas kernels: 0 us -> 515 us
  matrix products: 205 us -> 0 us
  local copies, waits for them, and re-layouts: 186 us -> 16.1 us
  other arithmetic: 54.7 us -> 1.95 us
  between operations: 14.1 us -> 0.02 us
    pallas_call x0 -> x2, Pallas kernels: none -> 515 us  [the longest x1 474 us: main_call(): pl.pallas_call(functools.partial(main_kernel, nc), in_specs=[any_spec] *...]
    all_gather x2 -> x0, waiting for transfers between devices: 506 us -> none  [the longest x1 340 us: tile_program(): right_full = lax.all_gather(right_moved, 'row', axis=2, tiled=True)]
    dot_general x4 -> x0, matrix products: 205 us -> none  [the longest x1 139 us: tile_program(): jnp.einsum('cin,crpn->cipr', left_full, right_full, preferred_element_typ...]
    ppermute x1 -> x0, waiting for transfers between devices: 197 us -> none  [tile_program(): right_moved = lax.ppermute(right_op, ('col', 'row'), swap_pairs)]
    reshape x2 -> x0, local copies, waits for them, and re-layouts: 185 us -> none  [the longest x1 162 us: tile_program(): right_full = right_full.reshape(hidden, tile_rows, row_ratio, seq_len)]
    convert_element_type x4 -> x0, other arithmetic: 29.3 us -> none  [the longest x1 29.2 us: tile_front(): (keep_f * jax.nn.sigmoid(projected[hidden:2 * hidden]) * projected[:hidde...]
    reduce_sum x3 -> x0, other arithmetic: 25.3 us -> none  [the longest x2 18 us: layer_norm(): spread = jnp.mean(centre * centre, axis=red_axis, keepdims=True)]
    unnamed x30 -> x7, local copies, waits for them, and re-layouts: 0.06 us -> 14.7 us
  transfers between devices with their start and end apart: 3 -> 0, of which waited for: 3 -> 0; matrix products, arithmetic and copies ran while one was open for 14% -> 0% of each run, Pallas kernels for 0% -> 0%
where the time goes in v1:
time: 534 us; the launch traced here: 533 us
  Pallas kernels  515 us (96%)
  local copies, waits for them, and re-layouts  16.1 us (3%)
    pallas_call x1, Pallas kernels, main_call(): pl.pallas_call(functools.partial(main_kernel, nc), in_specs=[any_spec] *...  474 us
    pallas_call x1, Pallas kernels, front(): pl.pallas_call(front_kernel, grid=(rows // fr,), in_specs=[pl.BlockSpec((...  41.2 us
    unnamed x7, local copies, waits for them, and re-layouts  14.7 us

profile of v1, /device:TPU:97, one launch (start us, length us, event | category | flops | bytes accessed | tf_op | source)
XLA Modules:
  0.0 533.4 jit_solution(5689602410615038312)
XLA Ops:
  0.0 0.7 bitcast_convert_fusion.1
  0.7 0.7 bitcast_convert_fusion
  1.3 0.8 copy.11
  2.1 0.8 copy.12
  2.9 0.8 copy.13
  3.7 0.8 copy.14
  4.6 0.6 maximum_bitcast_fusion.w_ref
  5.2 1.4 copy.16
  6.6 1.4 copy.17
  8.0 0.7 copy.15.g_ref.g_in
  8.7 0.7 copy.19.g_out
  9.4 41.2 %front.1 = (bf16[64,192,384]{2,1,0:T(8,128)(2,1)}, bf16[64,192,384]{2,1,0:T(8,128)(2,1)}) custom-call(bf16[192,64,384]{2,1,0:T(8,128)(2,1)} %bitcast.12, s32[192,384]{1,0:T(8,128)} %m_ref.1, f32[64,1]{1,0:T(8,128)} %copy.15.g_ref.g_in, bf16[256,64]{1,0:T(8,128)(2,1)} %maximum_bitcast_fusion.w_ref), custom_call_target="tpu_custom_call" | custom-call | tf_op jit(solution)/shard_map/front/pallas_call | solution.py:62
  50.6 474.2 %exchange.1 = (bf16[192,64,384]{2,1,0:T(8,128)(2,1)}, bf16[192,192,384]{2,1,0:T(8,128)(2,1)}, bf16[640,192,384]{2,1,0:T(8,128)(2,1)}) custom-call(bf16[64,192,384]{2,1,0:T(8,128)(2,1)} %get-tuple-element.8.a_own, bf16[64,192,384]{2,1,0:T(8,128)(2,1)} %get-tuple-element.9.b_own, bf16[192,64,384]{2,1,0:T(8,128)(2,1)} %bitcast.13, f32[64,1]{1,0:T(8,128)} %copy.15.g_ref.g_in, ...), custom_call_target="tpu_custom_call" | custom-call | tf_op jit(solution)/shard_map/exchange/pallas_call | solution.py:326
  524.8 8.7 %copy.21 = bf16[192,384,64]{1,2,0:T(8,128)(2,1)} copy(bf16[192,384,64]{1,2,0:T(8,128)(2,1)} %bitcast.14) | data formatting | bytes 18874368

commit v2 on v1

--- a/solution.py
+++ b/solution.py
@@ -11,9 +11,10 @@
 F32 = jnp.float32
 BF16 = jnp.bfloat16
 MESH = pl.DeviceIdType.MESH
-VMEM_LIMIT = 60 * 1024 * 1024
+VMEM_LIMIT = 66_000_000
 PER_HALF = 1
-FRONT_ROWS = 16
+GROUP = 8
+BLOCK = 16
 
 
 def normalize(values, gain):
@@ -22,63 +23,10 @@
     return (centre * lax.rsqrt(spread + LN_EPS) * gain).astype(BF16)
 
 
-def front_kernel(z_ref, m_ref, g_ref, w_ref, a_ref, b_ref, sa, sb):
-    rows, chan, cols = z_ref.shape
-    tiles = sa.shape[0]
-    pitch = sa.shape[1] // rows
-    hid = w_ref.shape[0] // 4
-
-    def one_row(i, _):
-        xn = normalize(z_ref[i].astype(F32), g_ref[...])
-        p = jnp.dot(w_ref[...], xn, preferred_element_type=F32)
-        keep = m_ref[pl.ds(i, 1), :].astype(F32)
-        left = keep * jax.nn.sigmoid(p[hid:2 * hid]) * p[:hid]
-        right = keep * jax.nn.sigmoid(p[3 * hid:]) * p[2 * hid:3 * hid]
-        at = pl.ds(pl.multiple_of(i * pitch, 8), hid)
-        for t in range(tiles):
-            sa[t, at, :] = left[:, t * 128:(t + 1) * 128]
-            sb[t, at, :] = right[:, t * 128:(t + 1) * 128]
-        return 0
-
-    lax.fori_loop(0, rows, one_row, 0, unroll=2)
-
-    def one_channel(c, _):
-        for t in range(tiles):
-            at = slice(t * 128, (t + 1) * 128)
-            a_ref[c, :, at] = sa[t, pl.ds(c, rows, stride=pitch), :].astype(BF16)
-            b_ref[c, :, at] = sb[t, pl.ds(c, rows, stride=pitch), :].astype(BF16)
-        return 0
-
-    lax.fori_loop(0, hid, one_channel, 0, unroll=4)
-
-
-def front(z_t, mask, g_in, w_cat):
-    rows, chan, cols = z_t.shape
-    hid = w_cat.shape[0] // 4
-    fr = FRONT_ROWS
-    scratch = pltpu.VMEM((cols // 128, fr * (hid + 8), 128), F32)
-    out = jax.ShapeDtypeStruct((hid, rows, cols), BF16)
-    out_spec = pl.BlockSpec((hid, fr, cols), lambda i: (0, i, 0))
-    return pl.pallas_call(
-        front_kernel,
-        grid=(rows // fr,),
-        in_specs=[
-            pl.BlockSpec((fr, chan, cols), lambda i: (i, 0, 0)),
-            pl.BlockSpec((fr, cols), lambda i: (i, 0)),
-            pl.BlockSpec((chan, 1), lambda i: (0, 0)),
-            pl.BlockSpec(w_cat.shape, lambda i: (0, 0)),
-        ],
-        out_specs=[out_spec, out_spec],
-        out_shape=[out, out],
-        scratch_shapes=[scratch, scratch],
-        compiler_params=pltpu.CompilerParams(vmem_limit_bytes=VMEM_LIMIT),
-        name="front",
-    )(z_t, mask, g_in, w_cat)
-
-
-def main_kernel(nc, a_own, b_own, z_hbm, g_in, w_gate, g_out, w_out, out_hbm, a_land, b_land,
-                a_buf, b_buf, o_buf, z_buf, sem_sp, sem_rp, sem_sa, sem_ra, sem_se, sem_re,
-                sem_sd, sem_rd, sem_l, sem_z):
+def main_kernel(nc, z_hbm, mask, norm_in, proj_left, gate_left, proj_right, gate_right, proj_gate, norm_out,
+                proj_out, out_hbm, a_own, b_own, a_land, b_land,
+                a_buf, b_buf, o_buf, z_buf, s_buf, stage_a, stage_b, turn, w_front, w_gate, w_out, g_in, g_out, sem_sp, sem_rp, sem_sa, sem_ra, sem_se, sem_re,
+                sem_sd, sem_rd, sem_l, sem_z, sem_in, sem_st):
     hid, rows, cols = a_own.shape
     h = PER_HALF
     ch = 2 * h
@@ -101,10 +49,73 @@
     barrier = pltpu.get_barrier_semaphore()
     for dev in (xp, xm, yp, ym, mate):
         pl.semaphore_signal(barrier, inc=1, device_id=dev, device_id_type=MESH)
+
+    parts = GROUP // ch
+    part_rows = rows // parts
+    groups = hid // GROUP
+    tiles = cols // 128
+    turn_pitch = turn.shape[1] // BLOCK
+
+    def first_load(p):
+        at = pl.ds(p * part_rows, part_rows)
+        return pltpu.make_async_copy(z_hbm.at[at], z_buf.at[at], sem_in.at[p])
+
+    for p in range(parts):
+        first_load(p).start()
+    for k, w in enumerate((proj_left, gate_left, proj_right, gate_right)):
+        w_t = w[...].astype(F32).T
+        for g in range(groups):
+            w_front[g, k * GROUP:(k + 1) * GROUP, :] = w_t[g * GROUP:(g + 1) * GROUP]
+    w_gate[...] = proj_gate[...].astype(F32).T.astype(BF16)
+    w_out[...] = proj_out[...].astype(F32).T.astype(BF16)
+    g_in[...] = jnp.broadcast_to(norm_in[...].astype(F32), (g_in.shape[0], g_in.shape[0])).T
+    g_out[...] = jnp.broadcast_to(norm_out[...].astype(F32), (g_out.shape[0], g_out.shape[0])).T
+
+    def front_part(g, p, first=False):
+        w = w_front[g].astype(BF16)
+
+        def block(blk, _):
+            def row(i, _):
+                r_i = blk * BLOCK + i
+                xn = z_buf[r_i]
+                if first:
+                    xn = normalize(xn.astype(F32), g_in[:, :1])
+                    z_buf[r_i] = xn
+                v = jnp.dot(w, xn, preferred_element_type=F32)
+                keep = mask[pl.ds(r_i, 1), :].astype(F32)
+                left = keep * jax.nn.sigmoid(v[GROUP:2 * GROUP]) * v[:GROUP]
+                right = keep * jax.nn.sigmoid(v[3 * GROUP:]) * v[2 * GROUP:3 * GROUP]
+                at = pl.multiple_of(i * turn_pitch, 8)
+                for j in range(tiles):
+                    turn[j, pl.ds(at, GROUP), :] = left[:, j * 128:(j + 1) * 128]
+                    turn[j, pl.ds(at + GROUP, GROUP), :] = right[:, j * 128:(j + 1) * 128]
+                return 0
+
+            lax.fori_loop(0, BLOCK, row, 0, unroll=4)
+            to = pl.ds(pl.multiple_of(blk * BLOCK, BLOCK), BLOCK)
+            for c in range(GROUP):
+                for j in range(tiles):
+                    at = slice(j * 128, (j + 1) * 128)
+                    stage_a[g % 2, c, to, at] = turn[j, pl.ds(c, BLOCK, stride=turn_pitch), :].astype(BF16)
+                    stage_b[g % 2, c, to, at] = turn[j, pl.ds(GROUP + c, BLOCK, stride=turn_pitch), :].astype(BF16)
+            return 0
+
+        per = part_rows // BLOCK
+        lax.fori_loop(p * per, (p + 1) * per, block, 0)
+
+    def stage_out(g):
+        to = pl.ds(g * GROUP, GROUP)
+        return [
+            pltpu.make_async_copy(stage_a.at[g % 2], a_own.at[to], sem_st.at[0, g % 2]),
+            pltpu.make_async_copy(stage_b.at[g % 2], b_own.at[to], sem_st.at[1, g % 2]),
+        ]
+
+    for p in range(parts):
+        first_load(p).wait()
+        front_part(0, p, first=True)
+    for c in stage_out(0):
+        c.start()
     pl.semaphore_wait(barrier, 5)
-
-    load_z = pltpu.make_async_copy(z_hbm, z_buf, sem_z.at[0])
-    load_z.start()
 
     dirs = [pick(1, 3, 0, 2), pick(0, 1, 1, 0), pick(2, 0, 3, 1), pick(3, 2, 2, 3)]
     hops = [pick(2, 1, 1, 1), pick(2, 1, 1, 1), pick(3, 2, 2, 2), pick(3, 4, 2, 4)]
@@ -181,7 +192,19 @@
         def _():
             fn(t)
 
+    gate_rows = rows // (n - 2 * parts)
+
+    def gate_row(first, j, _):
+        i = first + j
+        s_buf[i] = jax.nn.sigmoid(jnp.dot(w_gate[...], z_buf[i], preferred_element_type=F32))
+        return 0
+
     def step(q, _):
+        @pl.when(jnp.logical_and(q < n, q % parts == 0))
+        def _():
+            for c in stage_out(q // parts):
+                c.wait()
+
         for k in range(4):
             def send(t, k=k):
                 if k < 2:
@@ -278,21 +301,36 @@
                     o_buf[j, at, :] = prod[:, j * 128:(j + 1) * 128]
 
         at_lag(q, 8, multiply)
+
+        @pl.when(q < n - parts)
+        def _():
+            front_part(q // parts + 1, q % parts)
+
+            @pl.when(q % parts == parts - 1)
+            def _():
+                for c in stage_out(q // parts + 1):
+                    c.start()
+
+        @pl.when(q < n - 2 * parts)
+        def _():
+            lax.fori_loop(0, gate_rows, functools.partial(gate_row, q * gate_rows), 0, unroll=4)
+
+        @pl.when(q == n - parts)
+        def _():
+            pltpu.make_async_copy(z_hbm, z_buf, sem_z.at[0]).start()
+
         return 0
 
     lax.fori_loop(0, n + 8, step, 0)
 
-    load_z.wait()
+    pltpu.make_async_copy(z_hbm, z_buf, sem_z.at[0]).wait()
     pitch = o_buf.shape[1] // hid
 
     def back_row(i, _):
-        z = z_buf[i].astype(F32)
-        xn = normalize(z, g_in[...])
-        gate = jax.nn.sigmoid(jnp.dot(w_gate[...], xn, preferred_element_type=F32))
         o = jnp.concatenate([o_buf[j, pl.ds(i, hid, stride=pitch), :] for j in range(o_buf.shape[0])], axis=1)
-        on = normalize(o, g_out[...])
+        on = normalize(o, g_out[:, :1])
         update = jnp.dot(w_out[...], on, preferred_element_type=F32)
-        z_buf[i] = (z + gate * update).astype(BF16)
+        z_buf[i] = (z_buf[i].astype(F32) + s_buf[i] * update).astype(BF16)
         return 0
 
     per = rows // 8
@@ -315,9 +353,9 @@
         pltpu.make_async_copy(z_buf.at[pl.ds(blk * per, per)], out_hbm.at[pl.ds(blk * per, per)], sem_z.at[1 + blk]).wait()
 
 
-def main_call(nc, a_own, b_own, z_t, g_in, w_gate, g_out, w_out):
-    hid, rows, cols = a_own.shape
-    chan = z_t.shape[1]
+def main_call(nc, z_t, mask, small):
+    rows, chan, cols = z_t.shape
+    hid = chan
     ch = 2 * PER_HALF
     n = hid // ch
     any_spec = pl.BlockSpec(memory_space=pl.ANY)
@@ -325,10 +363,12 @@
     dma = lambda *s: pltpu.SemaphoreType.DMA(s)
     return pl.pallas_call(
         functools.partial(main_kernel, nc),
-        in_specs=[any_spec] * 3 + [vm] * 4,
-        out_specs=[any_spec] * 3,
+        in_specs=[any_spec] + [vm] * (1 + len(small)),
+        out_specs=[any_spec] * 5,
         out_shape=[
             jax.ShapeDtypeStruct(z_t.shape, BF16),
+            jax.ShapeDtypeStruct((hid, rows, cols), BF16),
+            jax.ShapeDtypeStruct((hid, rows, cols), BF16),
             jax.ShapeDtypeStruct((3 * hid, rows, cols), BF16),
             jax.ShapeDtypeStruct((10 * hid, rows, cols), BF16),
         ],
@@ -337,13 +377,22 @@
             pltpu.VMEM((2, ch, 2, rows, nc * cols), BF16),
             pltpu.VMEM((cols // 128, hid * (rows + 8), 128), F32),
             pltpu.VMEM(z_t.shape, BF16),
+            pltpu.VMEM(z_t.shape, F32),
+            pltpu.VMEM((2, GROUP, rows, cols), BF16),
+            pltpu.VMEM((2, GROUP, rows, cols), BF16),
+            pltpu.VMEM((cols // 128, BLOCK * (2 * GROUP + 8), 128), F32),
+            pltpu.VMEM((hid // GROUP, 4 * GROUP, chan), F32),
+            pltpu.VMEM((chan, chan), BF16),
+            pltpu.VMEM((chan, hid), BF16),
+            pltpu.VMEM((chan, chan), F32),
+            pltpu.VMEM((hid, hid), F32),
             dma(4, n), dma(6, n), dma(4, n), dma(4, n), dma(4, n), dma(4, n), dma(4, n), dma(4, n),
-            dma(2, 12), dma(9),
+            dma(2, 12), dma(9), dma(GROUP // ch), dma(2, 2),
         ],
         compiler_params=pltpu.CompilerParams(
             vmem_limit_bytes=VMEM_LIMIT, collective_id=0, has_side_effects=True),
         name="exchange",
-    )(a_own, b_own, z_t, g_in, w_gate, g_out, w_out)[0]
+    )(z_t, mask, *small)[0]
 
 
 def solution(mesh):
@@ -353,11 +402,7 @@
 
     def tile_program(pair_tile, mask_tile, norm_in, proj_left, gate_left, proj_right, gate_right, proj_gate, norm_out, proj_out):
         z_t = jnp.transpose(pair_tile, (0, 2, 1))
-        w_cat = jnp.concatenate([proj_left, gate_left, proj_right, gate_right], axis=1).T
-        g_in = norm_in.astype(F32)[:, None]
-        g_out = norm_out.astype(F32)[:, None]
-        a_own, b_own = front(z_t, mask_tile, g_in, w_cat)
-        out = main_call(nc, a_own, b_own, z_t, g_in, proj_gate.T, g_out, proj_out.T)
-        return jnp.transpose(out, (0, 2, 1))
+        small = (norm_in[None, :], proj_left, gate_left, proj_right, gate_right, proj_gate, norm_out[None, :], proj_out)
+        return jnp.transpose(main_call(nc, z_t, mask_tile, small), (0, 2, 1))
 
     return jax.shard_map(tile_program, mesh=mesh, in_specs=(tile_spec, mask_spec) + (P(),) * 8, out_specs=tile_spec, check_vma=False)

time: 534 us -> 491 us (0.919)
  Pallas kernels: 515 us -> 483 us
  local copies, waits for them, and re-layouts: 16.1 us -> 8.65 us
    pallas_call x2 -> x1, Pallas kernels: 515 us -> 483 us  [main_call(): pl.pallas_call(functools.partial(main_kernel, nc), in_specs=[any_spec] +...]
    unnamed x7 -> x1, local copies, waits for them, and re-layouts: 14.7 us -> 8.65 us
where the time goes in v2:
time: 491 us
  Pallas kernels  483 us (98%)
  local copies, waits for them, and re-layouts  8.65 us (2%)
    pallas_call x1, Pallas kernels, main_call(): pl.pallas_call(functools.partial(main_kernel, nc), in_specs=[any_spec] +...  483 us

profile of v2, /device:TPU:97, one launch (start us, length us, event | category | flops | bytes accessed | tf_op | source)
XLA Modules:
  0.0 491.3 jit_solution(1930221740087562531)
XLA Ops:
  0.0 482.6 %exchange.1 = (bf16[192,64,384]{2,1,0:T(8,128)(2,1)}, bf16[64,192,384]{2,1,0:T(8,128)(2,1)}, bf16[64,192,384]{2,1,0:T(8,128)(2,1)}, bf16[192,192,384]{2,1,0:T(8,128)(2,1)}, bf16[640,192,384]{2,1,0:T(8,128)(2,1)}) custom-call(bf16[192,64,384]{2,1,0:T(8,128)(2,1)} %bitcast.4, s32[192,384]{1,0:T(8,128)} %mask.1, bf16[1,64]{1,0:T(2,128)(2,1)} %bitcast.6, ...), custom_call_target="tpu_custom_call" | custom-call | tf_op jit(solution)/shard_map/exchange/pallas_call | solution.py:364
  482.7 8.7 %copy.12 = bf16[192,384,64]{1,2,0:T(8,128)(2,1)} copy(bf16[192,384,64]{1,2,0:T(8,128)(2,1)} %bitcast.5) | data formatting | bytes 18874368

commit v3 on v2

--- a/solution.py
+++ b/solution.py
@@ -15,6 +15,9 @@
 PER_HALF = 1
 GROUP = 8
 BLOCK = 16
+FRONT_UNROLL = 16
+BACK_UNROLL = 12
+LEAD = 4
 
 
 def normalize(values, gain):
@@ -91,7 +94,7 @@
                     turn[j, pl.ds(at + GROUP, GROUP), :] = right[:, j * 128:(j + 1) * 128]
                 return 0
 
-            lax.fori_loop(0, BLOCK, row, 0, unroll=4)
+            lax.fori_loop(0, BLOCK, row, 0, unroll=FRONT_UNROLL)
             to = pl.ds(pl.multiple_of(blk * BLOCK, BLOCK), BLOCK)
             for c in range(GROUP):
                 for j in range(tiles):
@@ -199,10 +202,19 @@
         s_buf[i] = jax.nn.sigmoid(jnp.dot(w_gate[...], z_buf[i], preferred_element_type=F32))
         return 0
 
-    def step(q, _):
-        @pl.when(jnp.logical_and(q < n, q % parts == 0))
-        def _():
-            for c in stage_out(q // parts):
+    def drain(t):
+        for k in range(4):
+            pltpu.make_async_copy(own(b_own, t, h), own(b_own, t, h), sem_sp.at[k, t]).wait()
+            pltpu.make_async_copy(own(b_own, t), own(b_own, t), sem_sd.at[k, t]).wait()
+        for k in range(4):
+            cnt = ch if k < 2 else h
+            pltpu.make_async_copy(own(b_own, t, cnt), own(b_own, t, cnt), sem_sa.at[k, t]).wait()
+            pltpu.make_async_copy(own(b_own, t, cnt), own(b_own, t, cnt), sem_se.at[k, t]).wait()
+
+    def perm_step(v):
+        @pl.when(jnp.logical_and(v < n, v % parts == 0))
+        def _():
+            for c in stage_out(v // parts):
                 c.wait()
 
         for k in range(4):
@@ -220,7 +232,27 @@
                     got_perm(src_relay[k], t)
                     perm_copy(k, t, b_land.at[pl.ds(relay0 + src_relay[k] * half + t * h, h)]).start()
 
-            at_lag(q, hops[k] - 1, send)
+            at_lag(v, hops[k] - 1, send)
+
+    def front_step(v):
+        @pl.when(v < n - parts)
+        def _():
+            front_part(v // parts + 1, v % parts)
+
+            @pl.when(v % parts == parts - 1)
+            def _():
+                for c in stage_out(v // parts + 1):
+                    c.start()
+
+    def step(q, _):
+        early = q < LEAD
+        v0 = jnp.where(early, 2 * q, q + LEAD)
+        perm_step(v0)
+
+        @pl.when(early)
+        def _():
+            front_step(2 * q)
+            perm_step(2 * q + 1)
 
         def e_own(t):
             @pl.when(is0)
@@ -235,13 +267,13 @@
                 for c in e_own_sends(t, land(b_land, 0, t)):
                     c.start()
 
-        at_lag(q, 4, e_own)
+        at_lag(q, 2, e_own)
 
         def a_first(t):
             for c in a_own_sends(t):
                 c.start()
 
-        at_lag(q, 3, a_first)
+        at_lag(q, 2, a_first)
 
         def e_fwd(t):
             got(b_land, sem_re.at[0, t], ch)
@@ -259,14 +291,14 @@
             got(a_land, sem_ra.at[1, t], ch)
             remote(land(a_land, 1, t, 1, h), land(a_land, 2, t, 1, h), sem_sa.at[3, t], sem_ra.at[3, t], ym).start()
 
-        at_lag(q, 4, a_fwd)
+        at_lag(q, 5, a_fwd)
 
         def last_d2d(t):
             got(b_land, sem_re.at[2, t], h)
             got(b_land, sem_re.at[3, t], h)
             remote(land(b_land, 3, t), land(b_land, 7, t), sem_sd.at[3, t], sem_rd.at[3, t], mate).start()
 
-        at_lag(q, 6, last_d2d)
+        at_lag(q, 7, last_d2d)
 
         def load(t):
             got(a_land, sem_ra.at[2, t], h)
@@ -285,7 +317,7 @@
             def _():
                 own_e_load(t, slot, land(b_land, 0, t)).start()
 
-        at_lag(q, 7, load)
+        at_lag(q, 8, load)
 
         def multiply(t):
             slot = t % 2
@@ -300,16 +332,10 @@
                 for j in range(o_buf.shape[0]):
                     o_buf[j, at, :] = prod[:, j * 128:(j + 1) * 128]
 
-        at_lag(q, 8, multiply)
-
-        @pl.when(q < n - parts)
-        def _():
-            front_part(q // parts + 1, q % parts)
-
-            @pl.when(q % parts == parts - 1)
-            def _():
-                for c in stage_out(q // parts + 1):
-                    c.start()
+        at_lag(q, 9, multiply)
+        at_lag(q, 9, drain)
+
+        front_step(jnp.where(early, 2 * q + 1, q + LEAD))
 
         @pl.when(q < n - 2 * parts)
         def _():
@@ -321,7 +347,7 @@
 
         return 0
 
-    lax.fori_loop(0, n + 8, step, 0)
+    lax.fori_loop(0, n + 9, step, 0)
 
     pltpu.make_async_copy(z_hbm, z_buf, sem_z.at[0]).wait()
     pitch = o_buf.shape[1] // hid
@@ -335,20 +361,9 @@
 
     per = rows // 8
     for blk in range(8):
-        lax.fori_loop(blk * per, (blk + 1) * per, back_row, 0, unroll=2)
+        lax.fori_loop(blk * per, (blk + 1) * per, back_row, 0, unroll=BACK_UNROLL)
         pltpu.make_async_copy(z_buf.at[pl.ds(blk * per, per)], out_hbm.at[pl.ds(blk * per, per)], sem_z.at[1 + blk]).start()
 
-    def drain(t, _):
-        for k in range(4):
-            pltpu.make_async_copy(own(b_own, t, h), own(b_own, t, h), sem_sp.at[k, t]).wait()
-            pltpu.make_async_copy(own(b_own, t), own(b_own, t), sem_sd.at[k, t]).wait()
-        for k in range(4):
-            cnt = ch if k < 2 else h
-            pltpu.make_async_copy(own(b_own, t, cnt), own(b_own, t, cnt), sem_sa.at[k, t]).wait()
-            pltpu.make_async_copy(own(b_own, t, cnt), own(b_own, t, cnt), sem_se.at[k, t]).wait()
-        return 0
-
-    lax.fori_loop(0, n, drain, 0)
     for blk in range(8):
         pltpu.make_async_copy(z_buf.at[pl.ds(blk * per, per)], out_hbm.at[pl.ds(blk * per, per)], sem_z.at[1 + blk]).wait()
 

time: 491 us -> 470 us (0.957)
  Pallas kernels: 483 us -> 458 us
    pallas_call x1, Pallas kernels: 483 us -> 458 us  [main_call(): pl.pallas_call(functools.partial(main_kernel, nc), in_specs=[any_spec] +...]
where the time goes in v3:
time: 470 us; the launch traced here: 467 us
  Pallas kernels  458 us (97%)
  local copies, waits for them, and re-layouts  8.65 us (2%)
    pallas_call x1, Pallas kernels, main_call(): pl.pallas_call(functools.partial(main_kernel, nc), in_specs=[any_spec] +...  458 us

profile of v3, /device:TPU:97, one launch (start us, length us, event | category | flops | bytes accessed | tf_op | source)
XLA Modules:
  0.0 467.1 jit_solution(13792998352994522685)
XLA Ops:
  0.0 458.4 %exchange.1 = (bf16[192,64,384]{2,1,0:T(8,128)(2,1)}, bf16[64,192,384]{2,1,0:T(8,128)(2,1)}, bf16[64,192,384]{2,1,0:T(8,128)(2,1)}, bf16[192,192,384]{2,1,0:T(8,128)(2,1)}, bf16[640,192,384]{2,1,0:T(8,128)(2,1)}) custom-call(bf16[192,64,384]{2,1,0:T(8,128)(2,1)} %bitcast.4, s32[192,384]{1,0:T(8,128)} %mask.1, bf16[1,64]{1,0:T(2,128)(2,1)} %bitcast.6, ...), custom_call_target="tpu_custom_call" | custom-call | tf_op jit(solution)/shard_map/exchange/pallas_call | solution.py:379
  458.4 8.7 %copy.12 = bf16[192,384,64]{1,2,0:T(8,128)(2,1)} copy(bf16[192,384,64]{1,2,0:T(8,128)(2,1)} %bitcast.5) | data formatting | bytes 18874368

commit v4 on v3

--- a/solution.py
+++ b/solution.py
@@ -168,7 +168,7 @@
             remote(src, land(b_land, 4, t), sem_sd.at[0, t], sem_rd.at[0, t], mate),
         ]
 
-    def local_loads(t, slot):
+    def local_load(t, slot, j):
         put_a = lambda rel: a_buf.at[slot, :, :, pl.ds(rel * cols, cols)]
         out = [
             (own(a_own, t), put_a(0)),
@@ -182,7 +182,7 @@
             if k > 0:
                 out.append((land(b_land, k, t), b_buf.at[slot, :, core, :, where]))
             out.append((land(b_land, 4 + k, t), b_buf.at[slot, :, 1 - core, :, where]))
-        return [pltpu.make_async_copy(s, d, sem_l.at[slot, j]) for j, (s, d) in enumerate(out)]
+        return pltpu.make_async_copy(out[j][0], out[j][1], sem_l.at[slot, j])
 
     def own_e_load(t, slot, src):
         where = pl.ds(pl.multiple_of(cls * cols, 128), cols)
@@ -267,13 +267,13 @@
                 for c in e_own_sends(t, land(b_land, 0, t)):
                     c.start()
 
-        at_lag(q, 2, e_own)
+        at_lag(q, pick(0, 1, 2, 1), e_own)
 
         def a_first(t):
             for c in a_own_sends(t):
                 c.start()
 
-        at_lag(q, 2, a_first)
+        at_lag(q, 1, a_first)
 
         def e_fwd(t):
             got(b_land, sem_re.at[0, t], ch)
@@ -283,7 +283,7 @@
             remote(land(b_land, 2, t, 1, h), land(b_land, 3, t, 1, h), sem_se.at[3, t], sem_re.at[3, t], xm).start()
             remote(land(b_land, 2, t), land(b_land, 6, t), sem_sd.at[2, t], sem_rd.at[2, t], mate).start()
 
-        at_lag(q, 5, e_fwd)
+        at_lag(q, 4, e_fwd)
 
         def a_fwd(t):
             got(a_land, sem_ra.at[0, t], ch)
@@ -291,38 +291,45 @@
             got(a_land, sem_ra.at[1, t], ch)
             remote(land(a_land, 1, t, 1, h), land(a_land, 2, t, 1, h), sem_sa.at[3, t], sem_ra.at[3, t], ym).start()
 
-        at_lag(q, 5, a_fwd)
+        at_lag(q, 4, a_fwd)
 
         def last_d2d(t):
             got(b_land, sem_re.at[2, t], h)
             got(b_land, sem_re.at[3, t], h)
             remote(land(b_land, 3, t), land(b_land, 7, t), sem_sd.at[3, t], sem_rd.at[3, t], mate).start()
 
-        at_lag(q, 7, last_d2d)
-
-        def load(t):
+        at_lag(q, 6, last_d2d)
+
+        late = (3, 9, 10)
+
+        def load_late(t):
             got(a_land, sem_ra.at[2, t], h)
             got(a_land, sem_ra.at[3, t], h)
-            for k in range(4):
+            got(b_land, sem_rd.at[3, t], ch)
+            for j in late:
+                local_load(t, t % 2, j).start()
+
+        def load_early(t):
+            for k in range(3):
                 got(b_land, sem_rd.at[k, t], ch)
-            slot = t % 2
-            for c in local_loads(t, slot):
-                c.start()
+            for j in range(11):
+                if j not in late:
+                    local_load(t, t % 2, j).start()
 
             @pl.when(is0)
             def _():
-                own_e_load(t, slot, own(b_own, t)).start()
+                own_e_load(t, t % 2, own(b_own, t)).start()
 
             @pl.when(jnp.logical_not(is0))
             def _():
-                own_e_load(t, slot, land(b_land, 0, t)).start()
-
-        at_lag(q, 8, load)
+                own_e_load(t, t % 2, land(b_land, 0, t)).start()
+
+        at_lag(q, 7, load_late)
 
         def multiply(t):
             slot = t % 2
-            for c in local_loads(t, slot):
-                c.wait()
+            for j in range(11):
+                local_load(t, slot, j).wait()
             own_e_load(t, slot, land(b_land, 0, t)).wait()
             pitch = o_buf.shape[1] // hid
             for c in range(ch):
@@ -332,8 +339,9 @@
                 for j in range(o_buf.shape[0]):
                     o_buf[j, at, :] = prod[:, j * 128:(j + 1) * 128]
 
-        at_lag(q, 9, multiply)
-        at_lag(q, 9, drain)
+        at_lag(q, 8, multiply)
+        at_lag(q, 6, load_early)
+        at_lag(q, 8, drain)
 
         front_step(jnp.where(early, 2 * q + 1, q + LEAD))
 
@@ -347,7 +355,7 @@
 
         return 0
 
-    lax.fori_loop(0, n + 9, step, 0)
+    lax.fori_loop(0, n + 8, step, 0)
 
     pltpu.make_async_copy(z_hbm, z_buf, sem_z.at[0]).wait()
     pitch = o_buf.shape[1] // hid
@@ -410,6 +418,40 @@
     )(z_t, mask, *small)[0]
 
 
+def copy_kernel(src, dst, buf, sem_a, sem_b):
+    parts = sem_a.shape[0]
+    per = src.shape[0] // parts
+
+    def take(p):
+        at = pl.ds(p * per, per)
+        return pltpu.make_async_copy(src.at[at], buf.at[at], sem_a.at[p])
+
+    def put(p):
+        at = pl.ds(p * per, per)
+        return pltpu.make_async_copy(buf.at[at], dst.at[at], sem_b.at[p])
+
+    for p in range(parts):
+        take(p).start()
+    for p in range(parts):
+        take(p).wait()
+        put(p).start()
+    for p in range(parts):
+        put(p).wait()
+
+
+def copy_out(v):
+    parts = 16
+    return pl.pallas_call(
+        copy_kernel,
+        in_specs=[pl.BlockSpec(memory_space=pl.ANY)],
+        out_specs=pl.BlockSpec(memory_space=pl.ANY),
+        out_shape=jax.ShapeDtypeStruct(v.shape, v.dtype),
+        scratch_shapes=[pltpu.VMEM(v.shape, v.dtype), pltpu.SemaphoreType.DMA((parts,)), pltpu.SemaphoreType.DMA((parts,))],
+        compiler_params=pltpu.CompilerParams(vmem_limit_bytes=VMEM_LIMIT),
+        name="copy_out",
+    )(v)
+
+
 def solution(mesh):
     nc = mesh.shape['col']
     tile_spec = P(('dp', 'row'), 'col', None)
@@ -418,6 +460,6 @@
     def tile_program(pair_tile, mask_tile, norm_in, proj_left, gate_left, proj_right, gate_right, proj_gate, norm_out, proj_out):
         z_t = jnp.transpose(pair_tile, (0, 2, 1))
         small = (norm_in[None, :], proj_left, gate_left, proj_right, gate_right, proj_gate, norm_out[None, :], proj_out)
-        return jnp.transpose(main_call(nc, z_t, mask_tile, small), (0, 2, 1))
+        return jnp.transpose(copy_out(main_call(nc, z_t, mask_tile, small)), (0, 2, 1))
 
     return jax.shard_map(tile_program, mesh=mesh, in_specs=(tile_spec, mask_spec) + (P(),) * 8, out_specs=tile_spec, check_vma=False)

time: 470 us -> 467 us (level)
  local copies, waits for them, and re-layouts: 8.65 us -> 0 us
    unnamed x1 -> x0, local copies, waits for them, and re-layouts: 8.65 us -> none
    pallas_call x0 -> x1, Pallas kernels: none -> 7.4 us  [copy_out(): pl.pallas_call(copy_kernel, in_specs=[pl.BlockSpec(memory_space=pl.ANY)],...]
where the time goes in v4:
time: 467 us; the launch traced here: 462 us
  Pallas kernels  462 us (99%)
    pallas_call x1, Pallas kernels, main_call(): pl.pallas_call(functools.partial(main_kernel, nc), in_specs=[any_spec] +...  455 us

profile of v4, /device:TPU:97, one launch (start us, length us, event | category | flops | bytes accessed | tf_op | source)
XLA Modules:
  0.0 462.4 jit_solution(10124931416051464521)
XLA Ops:
  0.0 454.8 %exchange.1 = (bf16[192,64,384]{2,1,0:T(8,128)(2,1)}, bf16[64,192,384]{2,1,0:T(8,128)(2,1)}, bf16[64,192,384]{2,1,0:T(8,128)(2,1)}, bf16[192,192,384]{2,1,0:T(8,128)(2,1)}, bf16[640,192,384]{2,1,0:T(8,128)(2,1)}) custom-call(bf16[192,64,384]{2,1,0:T(8,128)(2,1)} %bitcast.4, s32[192,384]{1,0:T(8,128)} %mask.1, bf16[1,64]{1,0:T(2,128)(2,1)} %bitcast.5, ...), custom_call_target="tpu_custom_call" | custom-call | tf_op jit(solution)/shard_map/exchange/pallas_call | solution.py:387
  454.8 7.4 %copy_out.1 = bf16[192,64,384]{2,1,0:T(8,128)(2,1)} custom-call(bf16[192,64,384]{2,1,0:T(8,128)(2,1)} %get-tuple-element.6.src), custom_call_target="tpu_custom_call" | custom-call | tf_op jit(solution)/shard_map/copy_out/pallas_call | solution.py:444
